TPU v7x, 32 devices: a whole 2x2x4 slice. The times are simulated.
32 devices in a mesh: rows: 4 (over z), cols: 4 (over x, core), rep: 2 (over y).
Axes of the slice: x: 2, y: 2, z: 4, core: 2. Of those that a mesh axis runs over, the one named last changes fastest.
Arguments:
- matrix: float32 [16384, 8192], P(('rep', 'rows'), 'cols'), parts along dimension 0, may hold values from -0.0625 to 0.0625
- labels: int32 [16384], P(('rep', 'rows')), parts along dimension 0, may hold values from 0 to 1
- lambdas: float32 [64], P('rep'), parts along dimension 0, may hold values from 0.01 to 0.2
- x_prev: float32 [64, 8192], P('rep', 'cols'), parts along dimension 0, may hold values from -4 to 4
- w_prev: float32 [64, 8192], P('rep', 'cols'), parts along dimension 0, may hold values from -4 to 4
- p_prev: float32 [64, 8192], P('rep', 'cols'), parts along dimension 0, may hold values from -1.5 to 1.5
- z_prev: float32 [64, 8192], P('rep', 'rows'), parts along dimension 0, may hold values from -6 to 6
- u_prev: float32 [64, 8192], P('rep', 'rows'), parts along dimension 0, may hold values from -6 to 6
Outputs:
- coeffs: float32 [64, 8192], P('rep', 'cols'), parts along dimension 0
- sparse: float32 [64, 8192], P('rep', 'cols'), parts along dimension 0
- margins: float32 [64, 8192], P('rep', 'rows'), parts along dimension 0
- margin_dual: float32 [64, 8192], P('rep', 'rows'), parts along dimension 0
There are 2 independent parts, one for each index of `rep`. A program takes and returns all parts, laid end to end along the dimension named above; each array names one. Nothing has to cross between parts.
All inputs are finite; a program needn't handle non-finite values.
Results may differ from a plain program's by a relative error of at most 0.0003.
Values sent between devices are 32-bit elements; how exact they have to be, the bound alone decides.
A program may use at most 128 MiB of HBM per device.

v0:
```python
import jax
import jax.numpy as jnp
from jax import lax
from jax.sharding import PartitionSpec as P

ITERS = 2
CG_STEPS = 5
NEWTON_STEPS = 8


HIGH = lax.Precision.HIGHEST


def apply_rows(vec, matrix):
    return lax.dot_general(
        vec, matrix, (((1,), (1,)), ((), ())), precision=HIGH, preferred_element_type=jnp.float32
    )


def apply_cols(vec, matrix):
    return lax.dot_general(
        vec, matrix, (((1,), (0,)), ((), ())), precision=HIGH, preferred_element_type=jnp.float32
    )


def proximal(target, sign):
    margin = target
    for step in range(NEWTON_STEPS):
        grad = margin - target - sign * jax.nn.sigmoid(-sign * margin)
        hess = 1.0 + jax.nn.sigmoid(margin) * jax.nn.sigmoid(-margin)
        margin = margin - grad / hess
    return margin


def forward(vec, matrix):
    return lax.psum(apply_rows(vec, matrix), "cols")


def forward_with_norm(vec, matrix):
    return lax.psum((apply_rows(vec, matrix), jnp.sum(vec * vec, axis=1)), "cols")


def backward(vec, matrix):
    partial_sum = apply_cols(vec, matrix)
    return lax.psum(partial_sum, "rows")


def squared_norm(value):
    return lax.psum(jnp.sum(value * value, axis=1), "cols")


def cg_image(direction, matrix):
    mapped, dd_part = forward_with_norm(direction, matrix)
    sq_part = jnp.sum(mapped * mapped, axis=1)
    back, sq_total = lax.psum((apply_cols(mapped, matrix), sq_part), "rows")
    curv_value = dd_part + sq_total
    return (direction + back, curv_value)


def local(matrix, labels, lambdas, x_prev, w_prev, p_prev, z_prev, u_prev):
    sign = (2.0 * labels.astype(jnp.float32) - 1.0)[None, :]
    coeffs, sparse, dual = (x_prev, w_prev, p_prev)
    margins, margin_dual = (z_prev, u_prev)
    for outer in range(ITERS):
        resid = (
            sparse
            - dual
            - coeffs
            + backward(margins - margin_dual - forward(coeffs, matrix), matrix)
        )
        direction = resid
        norm_now = squared_norm(resid)
        for step in range(CG_STEPS):
            image, curv_value = cg_image(direction, matrix)
            alpha = norm_now / curv_value
            coeffs = coeffs + alpha[:, None] * direction
            resid = resid - alpha[:, None] * image
            if step + 1 < CG_STEPS:
                norm_next = squared_norm(resid)
                direction = resid + (norm_next / norm_now)[:, None] * direction
                norm_now = norm_next
        target = forward(coeffs, matrix) + margin_dual
        margins = proximal(target, sign)
        margin_dual = target - margins
        total = coeffs + dual
        sparse = jnp.sign(total) * jnp.maximum(jnp.abs(total) - lambdas[:, None], 0.0)
        dual = total - sparse
    return (coeffs, sparse, margins, margin_dual)


def solution(mesh):
    return jax.shard_map(
        local,
        mesh=mesh,
        in_specs=(
            P(("rep", "rows"), "cols"),
            P(("rep", "rows")),
            P("rep"),
            P("rep", "cols"),
            P("rep", "cols"),
            P("rep", "cols"),
            P("rep", "rows"),
            P("rep", "rows"),
        ),
        out_specs=(P("rep", "cols"), P("rep", "cols"), P("rep", "rows"), P("rep", "rows")),
        check_vma=False,
    )
```

profile of v0, /device:TPU:0, one launch (start us, length us, event | category | flops | bytes accessed | tf_op | source)
XLA Modules:
  0.0 1297.5 jit_solution(16217579853619619662)
XLA Ops:
  26.6 35.1 %all-reduce.24.cloned.1.call-done = f32[32,2048]{1,0:T(8,128)} async-done(((f32[32,2048]{1,0:T(8,128)}), f32[32,2048]{1,0:T(8,128)}) %all-reduce.24.cloned.1.call-update) | async-done | bytes 262160 | tf_op jit(solution)/shard_map/psum | solution.py:36
  75.8 35.3 %all-reduce.26.cloned.1.call-done = f32[32,2048]{1,0:T(8,128)} async-done(((f32[32,2048]{1,0:T(8,128)}), f32[32,2048]{1,0:T(8,128)}) %all-reduce.26.cloned.1.call-update) | async-done | bytes 262160 | tf_op jit(solution)/shard_map/psum | solution.py:45
  137.2 26.6 %all-reduce.28.cloned.1.call-done = f32[32,2048]{1,0:T(8,128)} async-done(((f32[32,2048]{1,0:T(8,128)}), f32[32,2048]{1,0:T(8,128)}) %all-reduce.28.cloned.1.call-update) | async-done | bytes 262160 | tf_op jit(solution)/shard_map/psum | solution.py:40
  191.7 23.6 %all-reduce.30.cloned.1.call-done = f32[32,2048]{1,0:T(8,128)} async-done(((f32[32,2048]{1,0:T(8,128)}), f32[32,2048]{1,0:T(8,128)}) %all-reduce.30.cloned.1.call-update) | async-done | bytes 262160 | tf_op jit(solution)/shard_map/psum | solution.py:55
  249.4 25.7 %all-reduce.32.cloned.1.call-done = f32[32,2048]{1,0:T(8,128)} async-done(((f32[32,2048]{1,0:T(8,128)}), f32[32,2048]{1,0:T(8,128)}) %all-reduce.32.cloned.1.call-update) | async-done | bytes 262160 | tf_op jit(solution)/shard_map/psum | solution.py:40
  303.0 23.6 %all-reduce.34.cloned.1.call-done = f32[32,2048]{1,0:T(8,128)} async-done(((f32[32,2048]{1,0:T(8,128)}), f32[32,2048]{1,0:T(8,128)}) %all-reduce.34.cloned.1.call-update) | async-done | bytes 262160 | tf_op jit(solution)/shard_map/psum | solution.py:55
  359.7 25.9 %all-reduce.36.cloned.1.call-done = f32[32,2048]{1,0:T(8,128)} async-done(((f32[32,2048]{1,0:T(8,128)}), f32[32,2048]{1,0:T(8,128)}) %all-reduce.36.cloned.1.call-update) | async-done | bytes 262160 | tf_op jit(solution)/shard_map/psum | solution.py:40
  413.6 23.6 %all-reduce.38.cloned.1.call-done = f32[32,2048]{1,0:T(8,128)} async-done(((f32[32,2048]{1,0:T(8,128)}), f32[32,2048]{1,0:T(8,128)}) %all-reduce.38.cloned.1.call-update) | async-done | bytes 262160 | tf_op jit(solution)/shard_map/psum | solution.py:55
  470.3 25.9 %all-reduce.40.cloned.1.call-done = f32[32,2048]{1,0:T(8,128)} async-done(((f32[32,2048]{1,0:T(8,128)}), f32[32,2048]{1,0:T(8,128)}) %all-reduce.40.cloned.1.call-update) | async-done | bytes 262160 | tf_op jit(solution)/shard_map/psum | solution.py:40
  524.1 23.6 %all-reduce.42.cloned.1.call-done = f32[32,2048]{1,0:T(8,128)} async-done(((f32[32,2048]{1,0:T(8,128)}), f32[32,2048]{1,0:T(8,128)}) %all-reduce.42.cloned.1.call-update) | async-done | bytes 262160 | tf_op jit(solution)/shard_map/psum | solution.py:55
  554.8 20.0 %fusion.7 = f32[32,2048]{1,0:T(8,128)} fusion(f32[2048,2048]{1,0:T(8,128)} %param.8, f32[32,2048]{1,0:T(8,128)S(1)} %get-tuple-element.22, f32[32,2048]{1,0:T(8,128)S(1)} %get-tuple-element.24, f32[32]{0:T(128)S(1)} %div.253), kind=kOutput, calls=%fused_computation.61 | convolution fusion | flops 1610743808 | bytes 17563776 | tf_op jit(solution)/shard_map/dot_general | solution.py:15
  581.7 25.7 %all-reduce.44.cloned.1.call-done = f32[32,2048]{1,0:T(8,128)} async-done(((f32[32,2048]{1,0:T(8,128)}), f32[32,2048]{1,0:T(8,128)}) %all-reduce.44.cloned.1.call-update) | async-done | bytes 262160 | tf_op jit(solution)/shard_map/psum | solution.py:40
  640.3 29.4 %all-reduce.46.cloned.1.call-done = f32[32,2048]{1,0:T(8,128)} async-done(((f32[32,2048]{1,0:T(8,128)}), f32[32,2048]{1,0:T(8,128)}) %all-reduce.46.cloned.1.call-update) | async-done | bytes 262160 | tf_op jit(solution)/shard_map/psum | solution.py:36
  689.1 35.3 %all-reduce.48.cloned.1.call-done = f32[32,2048]{1,0:T(8,128)} async-done(((f32[32,2048]{1,0:T(8,128)}), f32[32,2048]{1,0:T(8,128)}) %all-reduce.48.cloned.1.call-update) | async-done | bytes 262160 | tf_op jit(solution)/shard_map/psum | solution.py:45
  750.6 26.6 %all-reduce.50.cloned.1.call-done = f32[32,2048]{1,0:T(8,128)} async-done(((f32[32,2048]{1,0:T(8,128)}), f32[32,2048]{1,0:T(8,128)}) %all-reduce.50.cloned.1.call-update) | async-done | bytes 262160 | tf_op jit(solution)/shard_map/psum | solution.py:40
  805.1 23.6 %all-reduce.52.cloned.1.call-done = f32[32,2048]{1,0:T(8,128)} async-done(((f32[32,2048]{1,0:T(8,128)}), f32[32,2048]{1,0:T(8,128)}) %all-reduce.52.cloned.1.call-update) | async-done | bytes 262160 | tf_op jit(solution)/shard_map/psum | solution.py:55
  862.8 25.7 %all-reduce.54.cloned.1.call-done = f32[32,2048]{1,0:T(8,128)} async-done(((f32[32,2048]{1,0:T(8,128)}), f32[32,2048]{1,0:T(8,128)}) %all-reduce.54.cloned.1.call-update) | async-done | bytes 262160 | tf_op jit(solution)/shard_map/psum | solution.py:40
  916.4 23.6 %all-reduce.56.cloned.1.call-done = f32[32,2048]{1,0:T(8,128)} async-done(((f32[32,2048]{1,0:T(8,128)}), f32[32,2048]{1,0:T(8,128)}) %all-reduce.56.cloned.1.call-update) | async-done | bytes 262160 | tf_op jit(solution)/shard_map/psum | solution.py:55
  973.1 25.9 %all-reduce.58.cloned.1.call-done = f32[32,2048]{1,0:T(8,128)} async-done(((f32[32,2048]{1,0:T(8,128)}), f32[32,2048]{1,0:T(8,128)}) %all-reduce.58.cloned.1.call-update) | async-done | bytes 262160 | tf_op jit(solution)/shard_map/psum | solution.py:40
  1027.0 23.6 %all-reduce.60.cloned.1.call-done = f32[32,2048]{1,0:T(8,128)} async-done(((f32[32,2048]{1,0:T(8,128)}), f32[32,2048]{1,0:T(8,128)}) %all-reduce.60.cloned.1.call-update) | async-done | bytes 262160 | tf_op jit(solution)/shard_map/psum | solution.py:55
  1083.7 25.9 %all-reduce.62.cloned.1.call-done = f32[32,2048]{1,0:T(8,128)} async-done(((f32[32,2048]{1,0:T(8,128)}), f32[32,2048]{1,0:T(8,128)}) %all-reduce.62.cloned.1.call-update) | async-done | bytes 262160 | tf_op jit(solution)/shard_map/psum | solution.py:40
  1137.5 23.8 %all-reduce.64.cloned.1.call-done = f32[32,2048]{1,0:T(8,128)} async-done(((f32[32,2048]{1,0:T(8,128)}), f32[32,2048]{1,0:T(8,128)}) %all-reduce.64.cloned.1.call-update) | async-done | bytes 262160 | tf_op jit(solution)/shard_map/psum | solution.py:55
  1195.2 25.7 %all-reduce.66.cloned.1.call-done = f32[32,2048]{1,0:T(8,128)} async-done(((f32[32,2048]{1,0:T(8,128)}), f32[32,2048]{1,0:T(8,128)}) %all-reduce.66.cloned.1.call-update) | async-done | bytes 262160 | tf_op jit(solution)/shard_map/psum | solution.py:40
  1254.4 29.7 %all-reduce.68.cloned.1.call-done = f32[32,2048]{1,0:T(8,128)} async-done(((f32[32,2048]{1,0:T(8,128)}), f32[32,2048]{1,0:T(8,128)}) %all-reduce.68.cloned.1.call-update) | async-done | bytes 262160 | tf_op jit(solution)/shard_map/psum | solution.py:36
  (183 shorter events, 649.4 us)
Async XLA Ops:
  7.2 104.0 %copy-start.2 = (f32[32,2048]{1,0:T(8,128)S(1)}, f32[32,2048]{1,0:T(8,128)}, u32[]{:S(2)}) copy-start(f32[32,2048]{1,0:T(8,128)} %param.11) | copy-start | bytes 786436
  7.2 54.6 %all-reduce.24.cloned.1.call-start = ((), (), s32[]{:S(2)}) async-start(), calls=%async_computation | async-start | bytes 524288 | tf_op jit(solution)/shard_map/psum | solution.py:36
  26.6 84.5 %all-reduce.26.cloned.1.call-start = ((), (), s32[]{:S(2)}) async-start(), calls=%async_computation.1 | async-start | bytes 524288 | tf_op jit(solution)/shard_map/psum | solution.py:45
  75.6 88.2 %all-reduce.28.cloned.1.call-start = ((), (), s32[]{:S(2)}) async-start(), calls=%async_computation.2 | async-start | bytes 524288 | tf_op jit(solution)/shard_map/psum | solution.py:40
  131.5 83.8 %all-reduce.30.cloned.1.call-start = ((), (), s32[]{:S(2)}) async-start(), calls=%async_computation.3 | async-start | bytes 524288 | tf_op jit(solution)/shard_map/psum | solution.py:55
  179.7 95.4 %all-reduce.32.cloned.1.call-start = ((), (), s32[]{:S(2)}) async-start(), calls=%async_computation.4 | async-start | bytes 524288 | tf_op jit(solution)/shard_map/psum | solution.py:40
  242.5 84.1 %all-reduce.34.cloned.1.call-start = ((), (), s32[]{:S(2)}) async-start(), calls=%async_computation.5 | async-start | bytes 524288 | tf_op jit(solution)/shard_map/psum | solution.py:55
  291.0 94.6 %all-reduce.36.cloned.1.call-start = ((), (), s32[]{:S(2)}) async-start(), calls=%async_computation.6 | async-start | bytes 524288 | tf_op jit(solution)/shard_map/psum | solution.py:40
  353.1 84.1 %all-reduce.38.cloned.1.call-start = ((), (), s32[]{:S(2)}) async-start(), calls=%async_computation.7 | async-start | bytes 524288 | tf_op jit(solution)/shard_map/psum | solution.py:55
  401.6 94.6 %all-reduce.40.cloned.1.call-start = ((), (), s32[]{:S(2)}) async-start(), calls=%async_computation.8 | async-start | bytes 524288 | tf_op jit(solution)/shard_map/psum | solution.py:40
  463.6 84.1 %all-reduce.42.cloned.1.call-start = ((), (), s32[]{:S(2)}) async-start(), calls=%async_computation.9 | async-start | bytes 524288 | tf_op jit(solution)/shard_map/psum | solution.py:55
  512.1 95.2 %all-reduce.44.cloned.1.call-start = ((), (), s32[]{:S(2)}) async-start(), calls=%async_computation.10 | async-start | bytes 524288 | tf_op jit(solution)/shard_map/psum | solution.py:40
  574.8 94.9 %all-reduce.46.cloned.1.call-start = ((), (), s32[]{:S(2)}) async-start(), calls=%async_computation.11 | async-start | bytes 524288 | tf_op jit(solution)/shard_map/psum | solution.py:36
  640.1 84.4 %all-reduce.48.cloned.1.call-start = ((), (), s32[]{:S(2)}) async-start(), calls=%async_computation.12 | async-start | bytes 524288 | tf_op jit(solution)/shard_map/psum | solution.py:45
  688.9 88.3 %all-reduce.50.cloned.1.call-start = ((), (), s32[]{:S(2)}) async-start(), calls=%async_computation.13 | async-start | bytes 524288 | tf_op jit(solution)/shard_map/psum | solution.py:40
  744.9 83.8 %all-reduce.52.cloned.1.call-start = ((), (), s32[]{:S(2)}) async-start(), calls=%async_computation.14 | async-start | bytes 524288 | tf_op jit(solution)/shard_map/psum | solution.py:55
  793.1 95.4 %all-reduce.54.cloned.1.call-start = ((), (), s32[]{:S(2)}) async-start(), calls=%async_computation.15 | async-start | bytes 524288 | tf_op jit(solution)/shard_map/psum | solution.py:40
  855.9 84.1 %all-reduce.56.cloned.1.call-start = ((), (), s32[]{:S(2)}) async-start(), calls=%async_computation.16 | async-start | bytes 524288 | tf_op jit(solution)/shard_map/psum | solution.py:55
  904.4 94.6 %all-reduce.58.cloned.1.call-start = ((), (), s32[]{:S(2)}) async-start(), calls=%async_computation.17 | async-start | bytes 524288 | tf_op jit(solution)/shard_map/psum | solution.py:40
  966.5 84.1 %all-reduce.60.cloned.1.call-start = ((), (), s32[]{:S(2)}) async-start(), calls=%async_computation.18 | async-start | bytes 524288 | tf_op jit(solution)/shard_map/psum | solution.py:55
  1015.0 94.6 %all-reduce.62.cloned.1.call-start = ((), (), s32[]{:S(2)}) async-start(), calls=%async_computation.19 | async-start | bytes 524288 | tf_op jit(solution)/shard_map/psum | solution.py:40
  1077.0 84.2 %all-reduce.64.cloned.1.call-start = ((), (), s32[]{:S(2)}) async-start(), calls=%async_computation.20 | async-start | bytes 524288 | tf_op jit(solution)/shard_map/psum | solution.py:55
  1125.5 95.4 %all-reduce.66.cloned.1.call-start = ((), (), s32[]{:S(2)}) async-start(), calls=%async_computation.21 | async-start | bytes 524288 | tf_op jit(solution)/shard_map/psum | solution.py:40
  1188.3 95.8 %all-reduce.68.cloned.1.call-start = ((), (), s32[]{:S(2)}) async-start(), calls=%async_computation.22 | async-start | bytes 524288 | tf_op jit(solution)/shard_map/psum | solution.py:36
  (17 other events, 694.1 us)
Sparse Core Ops, SparseCore 0:
  26.7 35.0 all-reduce.23
  75.7 35.3 all-reduce.25
  131.6 32.1 all-reduce.27
  179.8 35.3 all-reduce.29
  242.6 32.4 all-reduce.31
  291.1 35.3 all-reduce.33
  353.2 32.3 all-reduce.35
  401.7 35.3 all-reduce.37
  463.8 32.3 all-reduce.39
  512.3 35.4 all-reduce.41
  574.9 32.4 all-reduce.43
  640.2 29.4 all-reduce.45
  689.0 35.3 all-reduce.47
  745.0 32.1 all-reduce.49
  793.2 35.3 all-reduce.51
  856.0 32.4 all-reduce.53
  904.5 35.3 all-reduce.55
  966.6 32.3 all-reduce.57
  1015.1 35.3 all-reduce.59
  1077.2 32.3 all-reduce.61
  1125.7 35.5 all-reduce.63
  1188.5 32.4 all-reduce.65
  1254.6 29.4 all-reduce.67
where the time goes:
time: 1310 us; the launch traced here: 1300 us
  waiting for transfers between devices  614 us (47%)
  matrix products  412 us (31%)
  blocking collectives  230 us (18%)
  other arithmetic  25.7 us (2%)
  between operations  14.8 us (1%)
    psum x10, waiting for transfers between devices, forward_with_norm(): lax.psum((apply_rows(vec, matrix), jnp.sum(vec * vec, axis=1)), 'cols')  260 us
    dot_general x13, matrix products, apply_rows(): lax.dot_general(vec, matrix, (((1,), (1,)), ((), ())), precision=HIGH, pr...  253 us
    psum x8, waiting for transfers between devices, cg_image(): back, sq_total = lax.psum((apply_cols(mapped, matrix), sq_part), 'rows')  189 us
    dot_general x10, matrix products, apply_cols(): lax.dot_general(vec, matrix, (((1,), (0,)), ((), ())), precision=HIGH, pr...  159 us
    psum x10, blocking collectives, cg_image(): back, sq_total = lax.psum((apply_cols(mapped, matrix), sq_part), 'rows')  118 us
    psum x3, waiting for transfers between devices, forward(): return lax.psum(apply_rows(vec, matrix), 'cols')  94.2 us
    psum x2, waiting for transfers between devices, backward(): return lax.psum(partial_sum, 'rows')  70.6 us
    psum x10, blocking collectives, squared_norm(): return lax.psum(jnp.sum(value * value, axis=1), 'cols')  58.7 us
  transfers between devices with their start and end apart: 23, of which 23 were waited for; matrix products, arithmetic and copies ran while one was open for 0% of the time, Pallas kernels for 0%

commit v1 on v0

v1 whole, which is shorter than its diff:
```python
import functools

import jax
import jax.numpy as jnp
from jax import lax
from jax.experimental import pallas as pl
from jax.experimental.pallas import tpu as pltpu
from jax.sharding import PartitionSpec as P

ITERS = 2
CG_STEPS = 5
NEWTON_STEPS = 8
TILE = 256
F32 = jnp.float32
BF16 = jnp.bfloat16
MESH = pl.DeviceIdType.MESH


def split(value):
    hi = value.astype(BF16)
    return hi, (value - hi.astype(F32)).astype(BF16)


class Group:
    def __init__(self, axis, n, part, land, full, note, notes, sems):
        self.axis, self.n = axis, n
        self.part, self.land, self.full, self.note, self.notes = part, land, full, note, notes
        self.send, self.recv = sems
        self.me = lax.axis_index(axis)
        self.width = part.shape[2]

    def peer(self, o):
        return lax.rem(self.me + 1 + o, self.n)

    def copy(self, kind, o, src, dst):
        return pltpu.make_async_remote_copy(
            src_ref=src,
            dst_ref=dst,
            send_sem=self.send.at[kind, o],
            recv_sem=self.recv.at[kind, o],
            device_id={self.axis: self.peer(o)},
            device_id_type=MESH,
        )

    def scatter(self, o):
        return self.copy(0, o, self.part.at[self.peer(o)], self.land.at[o])

    def gather(self, o):
        return self.copy(1, o, self.full.at[self.me], self.full.at[self.me])

    def tell(self, o):
        return self.copy(2, o, self.note, self.notes.at[o])

    def start_notes(self, value):
        self.note[...] = value
        for o in range(self.n - 1):
            self.tell(o).start()

    def finish_notes(self):
        total = self.note[...]
        for o in range(self.n - 1):
            self.tell(o).wait_recv()
            total = total + self.notes[o]
        for o in range(self.n - 1):
            self.tell(o).wait_send()
        return total

    def multiply(self, both, hi_ref, lo_ref):
        paths = both.shape[0] // 2
        step = min(TILE, self.width)

        def chunk(o, carry):
            owner = self.peer(o)
            for t in range(self.width // step):
                cols = pl.ds(pl.multiple_of(owner * self.width + t * step, 128), step)
                wide = jnp.dot(both[...], hi_ref[:, cols], preferred_element_type=F32)
                low = jnp.dot(both[0:paths, :], lo_ref[:, cols], preferred_element_type=F32)
                self.part[owner, :, t * step : (t + 1) * step] = wide[:paths] + wide[paths:] + low

            @pl.when(o < self.n - 1)
            def _():
                self.scatter(o).start()

            return carry

        lax.fori_loop(0, self.n, chunk, 0)

    def finish_sum(self):
        total = self.part[self.me]
        for o in range(self.n - 1):
            self.scatter(o).wait_recv()
            total = total + self.land[o]
        self.full[self.me] = total
        for o in range(self.n - 1):
            self.gather(o).start()
        for o in range(self.n - 1):
            self.scatter(o).wait_send()
        for o in range(self.n - 1):
            self.gather(o).wait()


def kernel(
    nc, nr, matrix, sign, lambdas, x_prev, w_prev, p_prev, z_prev, u_prev,
    coeffs, sparse, margins, mdual,
    a_hi, a_lo, t_hi, t_lo, stage, stage_sem, both_f, both_s,
    dual, resid, direction, image_of, mapped, scal,
    c_part, c_land, c_full, c_note, c_notes, c_send, c_recv,
    r_part, r_land, r_full, r_note, r_notes, r_send, r_recv,
):
    cols = Group("cols", nc, c_part, c_land, c_full, c_note, c_notes, (c_send, c_recv))
    rows = Group("rows", nr, r_part, r_land, r_full, r_note, r_notes, (r_send, r_recv))
    samples, features = matrix.shape
    paths = x_prev.shape[0]
    blocks = samples // TILE

    barrier = pltpu.get_barrier_semaphore()
    for group in (cols, rows):
        for o in range(group.n - 1):
            pl.semaphore_signal(
                barrier, inc=1, device_id={group.axis: group.peer(o)}, device_id_type=MESH
            )

    def load(i, slot):
        return pltpu.make_async_copy(
            matrix.at[pl.ds(pl.multiple_of(i * TILE, TILE), TILE)], stage.at[slot], stage_sem.at[slot]
        )

    load(0, 0).start()
    coeffs[...] = x_prev[...]
    sparse[...] = w_prev[...]
    dual[...] = p_prev[...]
    margins[...] = z_prev[...]
    mdual[...] = u_prev[...]
    resid[...] = x_prev[...]
    direction[...] = jnp.zeros_like(direction)
    mapped[...] = jnp.zeros_like(mapped)
    image_of[...] = jnp.zeros_like(image_of)
    scal[...] = jnp.ones_like(scal)
    lane = lax.broadcasted_iota(jnp.int32, (paths, 128), 1)

    def prepare(i, carry):
        slot = lax.rem(i, 2)
        load(i, slot).wait()

        @pl.when(i + 1 < blocks)
        def _():
            load(i + 1, 1 - slot).start()

        down = pl.ds(pl.multiple_of(i * TILE, TILE), TILE)

        def block(j, carry):
            across = pl.ds(pl.multiple_of(j * TILE, TILE), TILE)
            value = stage[slot, :, across]
            a_hi[down, across], a_lo[down, across] = split(value)
            t_hi[across, down], t_lo[across, down] = split(value.T)
            return carry

        return lax.fori_loop(0, features // TILE, block, carry)

    lax.fori_loop(0, blocks, prepare, 0)
    pl.semaphore_wait(barrier, cols.n + rows.n - 2)

    def spread(value):
        return jnp.broadcast_to(value, (paths, 128))

    def rowsum(value):
        return jnp.sum(value, axis=1, keepdims=True)

    def advance(alpha):
        coeffs[...] += alpha * direction[...]
        image_of[...] += alpha * mapped[...]

    def proximal():
        for c in range(cols.n):
            at = slice(c * cols.width, (c + 1) * cols.width)
            target = image_of[:, at] + mdual[:, at]
            sgn = sign[:, at]

            def newton(_, m):
                s = 1.0 / (1.0 + jnp.exp(sgn * m))
                return m - (m - target - sgn * s) / (1.0 + s * (1.0 - s))

            m = lax.fori_loop(0, NEWTON_STEPS, newton, target)
            margins[:, at] = m
            mdual[:, at] = target - m
        total = coeffs[...] + dual[...]
        lam = lambdas[...]
        clipped = jnp.minimum(jnp.maximum(total, -lam), lam)
        sparse[...] = total - clipped
        dual[...] = clipped

    last = ITERS * CG_STEPS

    def pair(k, carry):
        step = lax.rem(k + CG_STEPS - 1, CG_STEPS)
        first = jnp.logical_or(step == 0, k == 0)
        closing = jnp.logical_or(step == CG_STEPS - 1, k == 0)
        r = resid[...]
        both_f[0:paths, :], both_f[paths:, :] = split(r)
        rr, rd = rowsum(r * r), rowsum(r * direction[...])
        cols.start_notes(jnp.where(lane == 0, rr, rd))
        cols.multiply(both_f, t_hi, t_lo)
        notes = cols.finish_notes()
        rr, rd = spread(notes[:, 0:1]), spread(notes[:, 1:2])
        beta = jnp.where(first, 0.0, rr / scal[0])
        scal[1] = rr + 2.0 * beta * rd + beta * beta * scal[1]
        scal[0] = rr
        beta = beta[:, 0:1]
        cols.finish_sum()

        @pl.when(k == 0)
        def _():
            for c in range(cols.n):
                image_of[:, c * cols.width : (c + 1) * cols.width] = cols.full[c]

        @pl.when(k > 0)
        def _():
            direction[...] = resid[...] + beta * direction[...]
            for c in range(cols.n):
                at = slice(c * cols.width, (c + 1) * cols.width)
                mapped[:, at] = cols.full[c] + beta * mapped[:, at]

        m = mapped[...]
        rows.start_notes(spread(rowsum(m * m)))

        @pl.when(closing)
        def _():
            @pl.when(k > 0)
            def _():
                sq = rows.finish_notes()
                advance((scal[0] / (scal[1] + sq))[:, 0:1])
                proximal()
                direction[...] = jnp.zeros_like(direction)
                mapped[...] = jnp.zeros_like(mapped)

            @pl.when(k == 0)
            def _():
                rows.finish_notes()

            both_s[0:paths, :], both_s[paths:, :] = split(margins[...] - mdual[...] - image_of[...])

        @pl.when(jnp.logical_not(closing))
        def _():
            both_s[0:paths, :], both_s[paths:, :] = split(m)

        @pl.when(k < last)
        def _():
            rows.multiply(both_s, a_hi, a_lo)

            @pl.when(jnp.logical_not(closing))
            def _():
                sq = rows.finish_notes()
                alpha = scal[0] / (scal[1] + sq)
                scal[2] = alpha
                advance(alpha[:, 0:1])

            rows.finish_sum()

            @pl.when(closing)
            def _():
                for c in range(rows.n):
                    at = slice(c * rows.width, (c + 1) * rows.width)
                    resid[:, at] = sparse[:, at] - dual[:, at] - coeffs[:, at] + rows.full[c]

            @pl.when(jnp.logical_not(closing))
            def _():
                alpha = scal[2][:, 0:1]
                for c in range(rows.n):
                    at = slice(c * rows.width, (c + 1) * rows.width)
                    resid[:, at] = resid[:, at] - alpha * (direction[:, at] + rows.full[c])

        return carry

    lax.fori_loop(0, last + 1, pair, 0)


def local(nc, nr, matrix, labels, lambdas, x_prev, w_prev, p_prev, z_prev, u_prev):
    sign = (2.0 * labels.astype(F32) - 1.0)[None, :]
    samples, features = matrix.shape
    paths = x_prev.shape[0]
    fvec, svec = (paths, features), (paths, samples)

    def comm(n, length):
        width = length // n
        return [
            pltpu.VMEM((n, paths, width), F32),
            pltpu.VMEM((n - 1, paths, width), F32),
            pltpu.VMEM((n, paths, width), F32),
            pltpu.VMEM((paths, 128), F32),
            pltpu.VMEM((n - 1, paths, 128), F32),
            pltpu.SemaphoreType.DMA((3, n - 1)),
            pltpu.SemaphoreType.DMA((3, n - 1)),
        ]

    vmem = pl.BlockSpec(memory_space=pltpu.VMEM)
    return pl.pallas_call(
        functools.partial(kernel, nc, nr),
        out_shape=tuple(jax.ShapeDtypeStruct(s, F32) for s in (fvec, fvec, svec, svec)),
        in_specs=[pl.BlockSpec(memory_space=pl.ANY)] + [vmem] * 7,
        out_specs=(vmem,) * 4,
        scratch_shapes=[
            pltpu.VMEM((samples, features), BF16),
            pltpu.VMEM((samples, features), BF16),
            pltpu.VMEM((features, samples), BF16),
            pltpu.VMEM((features, samples), BF16),
            pltpu.VMEM((2, TILE, features), F32),
            pltpu.SemaphoreType.DMA((2,)),
            pltpu.VMEM((2 * paths, features), BF16),
            pltpu.VMEM((2 * paths, samples), BF16),
            pltpu.VMEM(fvec, F32),
            pltpu.VMEM(fvec, F32),
            pltpu.VMEM(fvec, F32),
            pltpu.VMEM(svec, F32),
            pltpu.VMEM(svec, F32),
            pltpu.VMEM((3, paths, 128), F32),
        ]
        + comm(nc, samples)
        + comm(nr, features),
        compiler_params=pltpu.CompilerParams(
            collective_id=0, has_side_effects=True, vmem_limit_bytes=60 * 1024 * 1024
        ),
    )(matrix, sign, lambdas[:, None], x_prev, w_prev, p_prev, z_prev, u_prev)


def solution(mesh):
    return jax.shard_map(
        functools.partial(local, mesh.shape["cols"], mesh.shape["rows"]),
        mesh=mesh,
        in_specs=(
            P(("rep", "rows"), "cols"),
            P(("rep", "rows")),
            P("rep"),
            P("rep", "cols"),
            P("rep", "cols"),
            P("rep", "cols"),
            P("rep", "rows"),
            P("rep", "rows"),
        ),
        out_specs=(P("rep", "cols"), P("rep", "cols"), P("rep", "rows"), P("rep", "rows")),
        check_vma=False,
    )
```

time: 1310 us -> 317 us (0.24)
  waiting for transfers between devices: 614 us -> 0 us
  matrix products: 412 us -> 0 us
  Pallas kernels: 0 us -> 307 us
  blocking collectives: 230 us -> 0 us
  other arithmetic: 25.7 us -> 1.3 us
  between operations: 14.8 us -> 0.64 us
    psum x23 -> x0, waiting for transfers between devices: 613 us -> none  [the longest x10 260 us: forward_with_norm(): lax.psum((apply_rows(vec, matrix), jnp.sum(vec * vec, axis=1)), 'cols')]
    dot_general x23 -> x0, matrix products: 412 us -> none  [the longest x13 253 us: apply_rows(): lax.dot_general(vec, matrix, (((1,), (1,)), ((), ())), precision=HIGH, pr...]
    pallas_call x0 -> x1, Pallas kernels: none -> 307 us  [local(): pl.pallas_call(functools.partial(kernel, nc, nr), out_shape=tuple((jax.Sh...]
    psum x28 -> x0, blocking collectives: 230 us -> none  [the longest x10 118 us: cg_image(): back, sq_total = lax.psum((apply_cols(mapped, matrix), sq_part), 'rows')]
    reduce_sum x28 -> x0, other arithmetic: 16.9 us -> none  [the longest x10 11.9 us: squared_norm(): return lax.psum(jnp.sum(value * value, axis=1), 'cols')]
  transfers between devices with their start and end apart: 23 -> 0, of which waited for: 23 -> 0; matrix products, arithmetic and copies ran while one was open for 0% -> 0% of each run, Pallas kernels for 0% -> 0%
where the time goes in v1:
time: 317 us
  Pallas kernels  307 us (97%)
  local copies, waits for them, and re-layouts  8.02 us (3%)
    pallas_call x1, Pallas kernels, local(): pl.pallas_call(functools.partial(kernel, nc, nr), out_shape=tuple((jax.Sh...  307 us
    unnamed x4, local copies, waits for them, and re-layouts  6.68 us

profile of v1, /device:TPU:0, one launch (start us, length us, event | category | flops | bytes accessed | tf_op | source)
XLA Modules:
  0.0 316.5 jit_solution(12466358276675205281)
XLA Ops:
  0.6 1.3 multiply_add_fusion
  1.9 1.3 copy.12.lambdas
  3.3 306.6 %shard_map.111 = (f32[32,2048]{1,0:T(8,128)}, f32[32,2048]{1,0:T(8,128)}, f32[32,2048]{1,0:T(8,128)}, f32[32,2048]{1,0:T(8,128)}) custom-call(f32[2048,2048]{1,0:T(8,128)} %matrix.1, f32[1,2048]{1,0:T(1,128)} %bitcast.2, f32[32,1]{1,0:T(8,128)} %copy.12.lambdas, f32[32,2048]{1,0:T(8,128)} %x_prev.1, f32[32,2048]{1,0:T(8,128)} %w_prev.1, f32[32,2048]{1,0:T(8,128)} %p_prev.1, ...), custom_call_target="tpu_custom_call" | custom-call | tf_op jit(solution)/shard_map/pallas_call | solution.py:296
  309.8 1.7 copy.17
  311.5 1.7 copy.18
  313.2 1.7 copy.19
  314.8 1.7 copy.20

commit v2 on v1

--- a/solution.py
+++ b/solution.py
@@ -11,6 +11,7 @@
 CG_STEPS = 5
 NEWTON_STEPS = 8
 TILE = 256
+LAG = 3
 F32 = jnp.float32
 BF16 = jnp.bfloat16
 MESH = pl.DeviceIdType.MESH
@@ -22,60 +23,75 @@
 
 
 class Group:
-    def __init__(self, axis, n, part, land, full, note, notes, sems):
+    def __init__(self, axis, n, part, land, full, note, notes, send, recv, tell_send, tell_recv):
         self.axis, self.n = axis, n
         self.part, self.land, self.full, self.note, self.notes = part, land, full, note, notes
-        self.send, self.recv = sems
+        self.send, self.recv = send, recv
+        self.tell_send, self.tell_recv = tell_send, tell_recv
         self.me = lax.axis_index(axis)
-        self.width = part.shape[2]
+        self.count, self.paths, self.width = part.shape
+
+    @staticmethod
+    def shape(n, length):
+        return (n, n - 1, length // n)
 
     def peer(self, o):
         return lax.rem(self.me + 1 + o, self.n)
 
-    def copy(self, kind, o, src, dst):
+    def copy(self, kind, o, src, dst, peer):
         return pltpu.make_async_remote_copy(
             src_ref=src,
             dst_ref=dst,
             send_sem=self.send.at[kind, o],
             recv_sem=self.recv.at[kind, o],
+            device_id={self.axis: peer},
+            device_id_type=MESH,
+        )
+
+    def scatter(self, o):
+        peer = self.peer(o)
+        return self.copy(0, o, self.part.at[peer], self.land.at[0, o], peer)
+
+    def gather(self, o):
+        return self.copy(1, o, self.full.at[self.me], self.full.at[self.me], self.peer(o))
+
+    def tell(self, turn, o):
+        return pltpu.make_async_remote_copy(
+            src_ref=self.note.at[turn],
+            dst_ref=self.notes.at[turn, o],
+            send_sem=self.tell_send.at[turn, o],
+            recv_sem=self.tell_recv.at[turn, o],
             device_id={self.axis: self.peer(o)},
             device_id_type=MESH,
         )
 
-    def scatter(self, o):
-        return self.copy(0, o, self.part.at[self.peer(o)], self.land.at[o])
-
-    def gather(self, o):
-        return self.copy(1, o, self.full.at[self.me], self.full.at[self.me])
-
-    def tell(self, o):
-        return self.copy(2, o, self.note, self.notes.at[o])
-
-    def start_notes(self, value):
-        self.note[...] = value
+    def start_notes(self, turn, value):
+        self.note[turn] = value
         for o in range(self.n - 1):
-            self.tell(o).start()
-
-    def finish_notes(self):
-        total = self.note[...]
+            self.tell(turn, o).start()
+
+    def finish_notes(self, turn):
         for o in range(self.n - 1):
-            self.tell(o).wait_recv()
-            total = total + self.notes[o]
-        for o in range(self.n - 1):
-            self.tell(o).wait_send()
+            self.tell(turn, o).wait()
+        total = jnp.zeros(self.note.shape[1:], F32)
+        for d in range(self.n):
+            term = self.note[turn]
+            for o in range(self.n - 1):
+                term = jnp.where(self.peer(self.n - 2 - o) == d, self.notes[turn, o], term)
+            total = total + term
         return total
 
-    def multiply(self, both, hi_ref, lo_ref):
-        paths = both.shape[0] // 2
-        step = min(TILE, self.width)
-
+    def product(self, both, hi_ref, lo_ref, owner):
+        paths, step = self.paths, min(TILE, self.width)
+        for t in range(self.width // step):
+            cols = pl.ds(pl.multiple_of(owner * self.width + t * step, 128), step)
+            wide = jnp.dot(both[...], hi_ref[:, cols], preferred_element_type=F32)
+            low = jnp.dot(both[0:paths, :], lo_ref[:, cols], preferred_element_type=F32)
+            self.part[owner, :, t * step : (t + 1) * step] = wide[:paths] + wide[paths:] + low
+
+    def multiply(self, both, hi_ref, lo_ref, between=None):
         def chunk(o, carry):
-            owner = self.peer(o)
-            for t in range(self.width // step):
-                cols = pl.ds(pl.multiple_of(owner * self.width + t * step, 128), step)
-                wide = jnp.dot(both[...], hi_ref[:, cols], preferred_element_type=F32)
-                low = jnp.dot(both[0:paths, :], lo_ref[:, cols], preferred_element_type=F32)
-                self.part[owner, :, t * step : (t + 1) * step] = wide[:paths] + wide[paths:] + low
+            self.product(both, hi_ref, lo_ref, self.peer(o))
 
             @pl.when(o < self.n - 1)
             def _():
@@ -84,12 +100,14 @@
             return carry
 
         lax.fori_loop(0, self.n, chunk, 0)
+        if between is not None:
+            between()
 
     def finish_sum(self):
         total = self.part[self.me]
         for o in range(self.n - 1):
             self.scatter(o).wait_recv()
-            total = total + self.land[o]
+            total = total + self.land[0, o]
         self.full[self.me] = total
         for o in range(self.n - 1):
             self.gather(o).start()
@@ -99,16 +117,148 @@
             self.gather(o).wait()
 
 
+class Pairs(Group):
+    @staticmethod
+    def shape(n, length):
+        return (length // TILE, length // TILE, TILE)
+
+    def partner(self):
+        return self.me + 1 - 2 * lax.rem(self.me, 2)
+
+    def near(self, o, src):
+        return self.copy(0, o, self.part.at[src], self.land.at[0, o], self.partner())
+
+    def far(self, o, src):
+        return self.copy(1, o, self.part.at[src], self.land.at[1, o], self.across())
+
+    def back(self, o, src):
+        return self.copy(2, o, self.full.at[src], self.full.at[src], self.partner())
+
+
+class Square(Pairs):
+    def across(self):
+        return lax.rem(self.me + 2, 4)
+
+    def multiply(self, both, hi_ref, lo_ref, between=None):
+        half = self.count // 2
+        core = lax.rem(self.me, 2)
+        mine, other = core * half, (1 - core) * half
+
+        def give(o, carry):
+            self.product(both, hi_ref, lo_ref, other + o)
+            self.near(o, other + o).start()
+            return carry
+
+        def keep(o, carry):
+            self.product(both, hi_ref, lo_ref, mine + o)
+            self.near(o, other + o).wait_recv()
+            self.part[mine + o] += self.land[0, o]
+            self.far(o, mine + o).start()
+            return carry
+
+        lax.fori_loop(0, half, give, 0)
+        if between is not None:
+            between()
+        lax.fori_loop(0, half, keep, 0)
+
+    def finish_sum(self):
+        half = self.count // 2
+        core = lax.rem(self.me, 2)
+        mine, other = core * half, (1 - core) * half
+
+        def total(o, carry):
+            self.far(o, mine + o).wait_recv()
+            self.full[mine + o] = self.part[mine + o] + self.land[1, o]
+            self.back(o, mine + o).start()
+            return carry
+
+        def settle(o, carry):
+            self.near(o, other + o).wait_send()
+            self.far(o, mine + o).wait_send()
+            self.back(o, mine + o).wait()
+            return carry
+
+        lax.fori_loop(0, half, total, 0)
+        lax.fori_loop(0, half, settle, 0)
+
+
+class Chain(Pairs):
+    def across(self):
+        return 3 - self.me
+
+    def inner(self):
+        return jnp.logical_or(self.me == 1, self.me == 2)
+
+    def multiply(self, both, hi_ref, lo_ref, between=None):
+        def chunk(o, carry):
+            self.product(both, hi_ref, lo_ref, o)
+
+            @pl.when(jnp.logical_not(self.inner()))
+            def _():
+                self.near(o, o).start()
+
+            return carry
+
+        lax.fori_loop(0, self.count, chunk, 0)
+        if between is not None:
+            between()
+
+    def finish_sum(self):
+        count = self.count
+
+        @pl.when(self.inner())
+        def _():
+            def relay(o, carry):
+                @pl.when(o < count)
+                def _():
+                    self.near(o, o).wait_recv()
+                    self.part[o] += self.land[0, o]
+                    self.far(o, o).start()
+
+                @pl.when(o >= LAG)
+                def _():
+                    p = o - LAG
+                    self.far(p, p).wait_recv()
+                    self.full[p] = self.part[p] + self.land[1, p]
+                    self.back(p, p).start()
+
+                return carry
+
+            def settle(o, carry):
+                self.far(o, o).wait_send()
+                self.back(o, o).wait_send()
+                return carry
+
+            lax.fori_loop(0, count + LAG, relay, 0)
+            lax.fori_loop(0, count, settle, 0)
+
+        @pl.when(jnp.logical_not(self.inner()))
+        def _():
+            def settle(o, carry):
+                self.near(o, o).wait_send()
+                self.back(o, o).wait_recv()
+                return carry
+
+            lax.fori_loop(0, count, settle, 0)
+
+
+def col_kind(n):
+    return Square if n == 4 else Group
+
+
+def row_kind(n):
+    return Chain if n == 4 else Group
+
+
 def kernel(
     nc, nr, matrix, sign, lambdas, x_prev, w_prev, p_prev, z_prev, u_prev,
     coeffs, sparse, margins, mdual,
     a_hi, a_lo, t_hi, t_lo, stage, stage_sem, both_f, both_s,
     dual, resid, direction, image_of, mapped, scal,
-    c_part, c_land, c_full, c_note, c_notes, c_send, c_recv,
-    r_part, r_land, r_full, r_note, r_notes, r_send, r_recv,
+    *comm,
 ):
-    cols = Group("cols", nc, c_part, c_land, c_full, c_note, c_notes, (c_send, c_recv))
-    rows = Group("rows", nr, r_part, r_land, r_full, r_note, r_notes, (r_send, r_recv))
+    cols = col_kind(nc)("cols", nc, *comm[:9])
+    rows = row_kind(nr)("rows", nr, *comm[9:])
     samples, features = matrix.shape
     paths = x_prev.shape[0]
     blocks = samples // TILE
@@ -171,7 +321,7 @@
         image_of[...] += alpha * mapped[...]
 
     def proximal():
-        for c in range(cols.n):
+        for c in range(cols.count):
             at = slice(c * cols.width, (c + 1) * cols.width)
             target = image_of[:, at] + mdual[:, at]
             sgn = sign[:, at]
@@ -198,36 +348,44 @@
         r = resid[...]
         both_f[0:paths, :], both_f[paths:, :] = split(r)
         rr, rd = rowsum(r * r), rowsum(r * direction[...])
-        cols.start_notes(jnp.where(lane == 0, rr, rd))
-        cols.multiply(both_f, t_hi, t_lo)
-        notes = cols.finish_notes()
-        rr, rd = spread(notes[:, 0:1]), spread(notes[:, 1:2])
-        beta = jnp.where(first, 0.0, rr / scal[0])
-        scal[1] = rr + 2.0 * beta * rd + beta * beta * scal[1]
-        scal[0] = rr
-        beta = beta[:, 0:1]
+        turn = lax.rem(k, 2)
+        cols.start_notes(turn, jnp.where(lane == 0, rr, rd))
+
+        def direction_step():
+            notes = cols.finish_notes(turn)
+            rr, rd = spread(notes[:, 0:1]), spread(notes[:, 1:2])
+            beta = jnp.where(first, 0.0, rr / scal[0])
+            scal[1] = rr + 2.0 * beta * rd + beta * beta * scal[1]
+            scal[0] = rr
+            scal[2] = beta
+
+            @pl.when(k > 0)
+            def _():
+                direction[...] = resid[...] + beta[:, 0:1] * direction[...]
+
+        cols.multiply(both_f, t_hi, t_lo, direction_step)
         cols.finish_sum()
 
         @pl.when(k == 0)
         def _():
-            for c in range(cols.n):
+            for c in range(cols.count):
                 image_of[:, c * cols.width : (c + 1) * cols.width] = cols.full[c]
 
         @pl.when(k > 0)
         def _():
-            direction[...] = resid[...] + beta * direction[...]
-            for c in range(cols.n):
+            beta = scal[2][:, 0:1]
+            for c in range(cols.count):
                 at = slice(c * cols.width, (c + 1) * cols.width)
                 mapped[:, at] = cols.full[c] + beta * mapped[:, at]
 
         m = mapped[...]
-        rows.start_notes(spread(rowsum(m * m)))
+        rows.start_notes(turn, spread(rowsum(m * m)))
 
         @pl.when(closing)
         def _():
             @pl.when(k > 0)
             def _():
-                sq = rows.finish_notes()
+                sq = rows.finish_notes(turn)
                 advance((scal[0] / (scal[1] + sq))[:, 0:1])
                 proximal()
                 direction[...] = jnp.zeros_like(direction)
@@ -235,7 +393,7 @@
 
             @pl.when(k == 0)
             def _():
-                rows.finish_notes()
+                rows.finish_notes(turn)
 
             both_s[0:paths, :], both_s[paths:, :] = split(margins[...] - mdual[...] - image_of[...])
 
@@ -245,27 +403,27 @@
 
         @pl.when(k < last)
         def _():
-            rows.multiply(both_s, a_hi, a_lo)
-
-            @pl.when(jnp.logical_not(closing))
-            def _():
-                sq = rows.finish_notes()
-                alpha = scal[0] / (scal[1] + sq)
-                scal[2] = alpha
-                advance(alpha[:, 0:1])
-
+            def length_step():
+                @pl.when(jnp.logical_not(closing))
+                def _():
+                    sq = rows.finish_notes(turn)
+                    alpha = scal[0] / (scal[1] + sq)
+                    scal[2] = alpha
+                    advance(alpha[:, 0:1])
+
+            rows.multiply(both_s, a_hi, a_lo, length_step)
             rows.finish_sum()
 
             @pl.when(closing)
             def _():
-                for c in range(rows.n):
+                for c in range(rows.count):
                     at = slice(c * rows.width, (c + 1) * rows.width)
                     resid[:, at] = sparse[:, at] - dual[:, at] - coeffs[:, at] + rows.full[c]
 
             @pl.when(jnp.logical_not(closing))
             def _():
                 alpha = scal[2][:, 0:1]
-                for c in range(rows.n):
+                for c in range(rows.count):
                     at = slice(c * rows.width, (c + 1) * rows.width)
                     resid[:, at] = resid[:, at] - alpha * (direction[:, at] + rows.full[c])
 
@@ -280,16 +438,18 @@
     paths = x_prev.shape[0]
     fvec, svec = (paths, features), (paths, samples)
 
-    def comm(n, length):
-        width = length // n
+    def comm(kind, n, length):
+        count, slots, width = kind.shape(n, length)
         return [
-            pltpu.VMEM((n, paths, width), F32),
-            pltpu.VMEM((n - 1, paths, width), F32),
-            pltpu.VMEM((n, paths, width), F32),
-            pltpu.VMEM((paths, 128), F32),
-            pltpu.VMEM((n - 1, paths, 128), F32),
-            pltpu.SemaphoreType.DMA((3, n - 1)),
-            pltpu.SemaphoreType.DMA((3, n - 1)),
+            pltpu.VMEM((count, paths, width), F32),
+            pltpu.VMEM((2, slots, paths, width), F32),
+            pltpu.VMEM((count, paths, width), F32),
+            pltpu.VMEM((2, paths, 128), F32),
+            pltpu.VMEM((2, n - 1, paths, 128), F32),
+            pltpu.SemaphoreType.DMA((3, slots)),
+            pltpu.SemaphoreType.DMA((3, slots)),
+            pltpu.SemaphoreType.DMA((2, n - 1)),
+            pltpu.SemaphoreType.DMA((2, n - 1)),
         ]
 
     vmem = pl.BlockSpec(memory_space=pltpu.VMEM)
@@ -314,8 +474,8 @@
             pltpu.VMEM(svec, F32),
             pltpu.VMEM((3, paths, 128), F32),
         ]
-        + comm(nc, samples)
-        + comm(nr, features),
+        + comm(col_kind(nc), nc, samples)
+        + comm(row_kind(nr), nr, features),
         compiler_params=pltpu.CompilerParams(
             collective_id=0, has_side_effects=True, vmem_limit_bytes=60 * 1024 * 1024
         ),

time: 317 us -> 305 us (0.962)
  Pallas kernels: 307 us -> 295 us
    pallas_call x1, Pallas kernels: 307 us -> 295 us  [local(): pl.pallas_call(functools.partial(kernel, nc, nr), out_shape=tuple((jax.Sh...]
where the time goes in v2:
time: 305 us; the launch traced here: 304 us
  Pallas kernels  295 us (97%)
  local copies, waits for them, and re-layouts  8.02 us (3%)
    pallas_call x1, Pallas kernels, local(): pl.pallas_call(functools.partial(kernel, nc, nr), out_shape=tuple((jax.Sh...  295 us
    unnamed x4, local copies, waits for them, and re-layouts  6.68 us

profile of v2, /device:TPU:0, one launch (start us, length us, event | category | flops | bytes accessed | tf_op | source)
XLA Modules:
  0.0 304.5 jit_solution(16449222497583716123)
XLA Ops:
  0.6 1.3 multiply_add_fusion
  1.9 1.3 copy.12.lambdas
  3.3 294.5 %shard_map.111 = (f32[32,2048]{1,0:T(8,128)}, f32[32,2048]{1,0:T(8,128)}, f32[32,2048]{1,0:T(8,128)}, f32[32,2048]{1,0:T(8,128)}) custom-call(f32[2048,2048]{1,0:T(8,128)} %matrix.1, f32[1,2048]{1,0:T(1,128)} %bitcast.2, f32[32,1]{1,0:T(8,128)} %copy.12.lambdas, f32[32,2048]{1,0:T(8,128)} %x_prev.1, f32[32,2048]{1,0:T(8,128)} %w_prev.1, f32[32,2048]{1,0:T(8,128)} %p_prev.1, ...), custom_call_target="tpu_custom_call" | custom-call | tf_op jit(solution)/shard_map/pallas_call | solution.py:456
  297.8 1.7 copy.17
  299.5 1.7 copy.18
  301.2 1.7 copy.19
  302.8 1.7 copy.20

commit v3 on v2

--- a/solution.py
+++ b/solution.py
@@ -11,6 +11,7 @@
 CG_STEPS = 5
 NEWTON_STEPS = 8
 TILE = 256
+CHUNK = 256
 LAG = 3
 F32 = jnp.float32
 BF16 = jnp.bfloat16
@@ -65,8 +66,9 @@
             device_id_type=MESH,
         )
 
-    def start_notes(self, turn, value):
-        self.note[turn] = value
+    def start_notes(self, turn, *values):
+        for i, value in enumerate(values):
+            self.note[turn, i : i + 1, :] = value
         for o in range(self.n - 1):
             self.tell(turn, o).start()
 
@@ -82,7 +84,7 @@
         return total
 
     def product(self, both, hi_ref, lo_ref, owner):
-        paths, step = self.paths, min(TILE, self.width)
+        paths, step = self.paths, min(CHUNK, self.width)
         for t in range(self.width // step):
             cols = pl.ds(pl.multiple_of(owner * self.width + t * step, 128), step)
             wide = jnp.dot(both[...], hi_ref[:, cols], preferred_element_type=F32)
@@ -120,7 +122,7 @@
 class Pairs(Group):
     @staticmethod
     def shape(n, length):
-        return (length // TILE, length // TILE, TILE)
+        return (length // CHUNK, length // CHUNK, CHUNK)
 
     def partner(self):
         return self.me + 1 - 2 * lax.rem(self.me, 2)
@@ -286,7 +288,10 @@
     mapped[...] = jnp.zeros_like(mapped)
     image_of[...] = jnp.zeros_like(image_of)
     scal[...] = jnp.ones_like(scal)
+    cols.note[...] = jnp.zeros_like(cols.note)
+    rows.note[...] = jnp.zeros_like(rows.note)
     lane = lax.broadcasted_iota(jnp.int32, (paths, 128), 1)
+    diagonal = lane == lax.broadcasted_iota(jnp.int32, (paths, 128), 0)
 
     def prepare(i, carry):
         slot = lax.rem(i, 2)
@@ -314,7 +319,11 @@
         return jnp.broadcast_to(value, (paths, 128))
 
     def rowsum(value):
-        return jnp.sum(value, axis=1, keepdims=True)
+        value = jnp.sum(value, axis=1, keepdims=True)
+        return jnp.sum(jnp.where(diagonal, value, 0.0), axis=0, keepdims=True)
+
+    def per_path(row):
+        return spread(jnp.sum(jnp.where(diagonal, row, 0.0), axis=1, keepdims=True))
 
     def advance(alpha):
         coeffs[...] += alpha * direction[...]
@@ -349,11 +358,11 @@
         both_f[0:paths, :], both_f[paths:, :] = split(r)
         rr, rd = rowsum(r * r), rowsum(r * direction[...])
         turn = lax.rem(k, 2)
-        cols.start_notes(turn, jnp.where(lane == 0, rr, rd))
+        cols.start_notes(turn, rr, rd)
 
         def direction_step():
             notes = cols.finish_notes(turn)
-            rr, rd = spread(notes[:, 0:1]), spread(notes[:, 1:2])
+            rr, rd = per_path(notes[0:1]), per_path(notes[1:2])
             beta = jnp.where(first, 0.0, rr / scal[0])
             scal[1] = rr + 2.0 * beta * rd + beta * beta * scal[1]
             scal[0] = rr
@@ -379,13 +388,13 @@
                 mapped[:, at] = cols.full[c] + beta * mapped[:, at]
 
         m = mapped[...]
-        rows.start_notes(turn, spread(rowsum(m * m)))
+        rows.start_notes(turn, rowsum(m * m))
 
         @pl.when(closing)
         def _():
             @pl.when(k > 0)
             def _():
-                sq = rows.finish_notes(turn)
+                sq = per_path(rows.finish_notes(turn)[0:1])
                 advance((scal[0] / (scal[1] + sq))[:, 0:1])
                 proximal()
                 direction[...] = jnp.zeros_like(direction)
@@ -406,7 +415,7 @@
             def length_step():
                 @pl.when(jnp.logical_not(closing))
                 def _():
-                    sq = rows.finish_notes(turn)
+                    sq = per_path(rows.finish_notes(turn)[0:1])
                     alpha = scal[0] / (scal[1] + sq)
                     scal[2] = alpha
                     advance(alpha[:, 0:1])
@@ -444,8 +453,8 @@
             pltpu.VMEM((count, paths, width), F32),
             pltpu.VMEM((2, slots, paths, width), F32),
             pltpu.VMEM((count, paths, width), F32),
-            pltpu.VMEM((2, paths, 128), F32),
-            pltpu.VMEM((2, n - 1, paths, 128), F32),
+            pltpu.VMEM((2, 8, 128), F32),
+            pltpu.VMEM((2, n - 1, 8, 128), F32),
             pltpu.SemaphoreType.DMA((3, slots)),
             pltpu.SemaphoreType.DMA((3, slots)),
             pltpu.SemaphoreType.DMA((2, n - 1)),

time: 305 us -> 297 us (0.974)
  Pallas kernels: 295 us -> 286 us
    pallas_call x1, Pallas kernels: 295 us -> 286 us  [local(): pl.pallas_call(functools.partial(kernel, nc, nr), out_shape=tuple((jax.Sh...]
where the time goes in v3:
time: 297 us; the launch traced here: 296 us
  Pallas kernels  286 us (96%)
  local copies, waits for them, and re-layouts  8.02 us (3%)
    pallas_call x1, Pallas kernels, local(): pl.pallas_call(functools.partial(kernel, nc, nr), out_shape=tuple((jax.Sh...  286 us
    unnamed x4, local copies, waits for them, and re-layouts  6.68 us

profile of v3, /device:TPU:0, one launch (start us, length us, event | category | flops | bytes accessed | tf_op | source)
XLA Modules:
  0.0 296.0 jit_solution(7188869906621338051)
XLA Ops:
  0.6 1.3 multiply_add_fusion
  1.9 1.3 copy.12.lambdas
  3.3 286.0 %shard_map.111 = (f32[32,2048]{1,0:T(8,128)}, f32[32,2048]{1,0:T(8,128)}, f32[32,2048]{1,0:T(8,128)}, f32[32,2048]{1,0:T(8,128)}) custom-call(f32[2048,2048]{1,0:T(8,128)} %matrix.1, f32[1,2048]{1,0:T(1,128)} %bitcast.2, f32[32,1]{1,0:T(8,128)} %copy.12.lambdas, f32[32,2048]{1,0:T(8,128)} %x_prev.1, f32[32,2048]{1,0:T(8,128)} %w_prev.1, f32[32,2048]{1,0:T(8,128)} %p_prev.1, ...), custom_call_target="tpu_custom_call" | custom-call | tf_op jit(solution)/shard_map/pallas_call | solution.py:465
  289.3 1.7 copy.17
  290.9 1.7 copy.18
  292.6 1.7 copy.19
  294.3 1.7 copy.20

commit v4 on v3

--- a/solution.py
+++ b/solution.py
@@ -310,7 +310,7 @@
             t_hi[across, down], t_lo[across, down] = split(value.T)
             return carry
 
-        return lax.fori_loop(0, features // TILE, block, carry)
+        return lax.fori_loop(0, features // TILE, block, carry, unroll=2)
 
     lax.fori_loop(0, blocks, prepare, 0)
     pl.semaphore_wait(barrier, cols.n + rows.n - 2)
@@ -330,8 +330,9 @@
         image_of[...] += alpha * mapped[...]
 
     def proximal():
-        for c in range(cols.count):
-            at = slice(c * cols.width, (c + 1) * cols.width)
+        piece = min(1024, samples)
+        for c in range(samples // piece):
+            at = slice(c * piece, (c + 1) * piece)
             target = image_of[:, at] + mdual[:, at]
             sgn = sign[:, at]
 

time: 297 us -> 295 us (level)
  no operation moved by 1% of the time
where the time goes in v4:
time: 295 us; the launch traced here: 294 us
  Pallas kernels  284 us (96%)
  local copies, waits for them, and re-layouts  8.02 us (3%)
    pallas_call x1, Pallas kernels, local(): pl.pallas_call(functools.partial(kernel, nc, nr), out_shape=tuple((jax.Sh...  284 us
    unnamed x4, local copies, waits for them, and re-layouts  6.68 us

profile of v4, /device:TPU:0, one launch (start us, length us, event | category | flops | bytes accessed | tf_op | source)
XLA Modules:
  0.0 294.4 jit_solution(17814536698779219672)
XLA Ops:
  0.6 1.3 multiply_add_fusion
  1.9 1.3 copy.12.lambdas
  3.3 284.4 %shard_map.111 = (f32[32,2048]{1,0:T(8,128)}, f32[32,2048]{1,0:T(8,128)}, f32[32,2048]{1,0:T(8,128)}, f32[32,2048]{1,0:T(8,128)}) custom-call(f32[2048,2048]{1,0:T(8,128)} %matrix.1, f32[1,2048]{1,0:T(1,128)} %bitcast.2, f32[32,1]{1,0:T(8,128)} %copy.12.lambdas, f32[32,2048]{1,0:T(8,128)} %x_prev.1, f32[32,2048]{1,0:T(8,128)} %w_prev.1, f32[32,2048]{1,0:T(8,128)} %p_prev.1, ...), custom_call_target="tpu_custom_call" | custom-call | tf_op jit(solution)/shard_map/pallas_call | solution.py:466
  287.7 1.7 copy.17
  289.3 1.7 copy.18
  291.0 1.7 copy.19
  292.7 1.7 copy.20
